TPU v7x, 32 devices: a whole 2x2x4 slice. The times are simulated.
32 devices in a mesh: batch: 8 (over z, x), mp: 4 (over y, core).
Axes of the slice: x: 2, y: 2, z: 4, core: 2. Of those that a mesh axis runs over, the one named last changes fastest.
Arguments:
- features: bfloat16 [1024, 65536], P('batch', 'mp'), may hold values from 0 to 4
- tiles: bfloat16 [2, 512, 3, 128, 128], P(None, 'mp', None, 'batch'), may hold values from -0.3125 to 0.3125
- biases: float32 [2, 65536], P(None, 'mp'), may hold values from -0.5 to 0
- in_block: int32 [2, 512, 3], replicated, may hold values from 0 to 511, as said below
Outputs:
- activations: bfloat16 [1024, 65536], P('batch', 'mp')
- row_means: float32 [1024], P('batch')
- grand: float32 [], replicated
Inputs may be any that keep to these rules, and one draw needn't show every extreme that they name: `in_block`: number the 384 tiles of mp shard m (column blocks m * 128 to (m + 1) * 128 - 1) in order of column block, then tile slot; tile number s reads a block of shard s // 96, that is an id in [(s // 96) * 128, (s // 96 + 1) * 128).
All inputs are finite; a program needn't handle non-finite values.
Results may differ from a plain program's by a relative error of at most 0.0052.
Values may be sent and summed in bfloat16 or wider, within the bound.
A program may use at most 128 MiB of HBM per device.

v0:
```python
import jax
import jax.numpy as jnp
from jax import lax
from jax.sharding import PartitionSpec as P

NEUR = 65536


def on_device(features, tiles, biases, in_block):
    shard_count = lax.axis_size("mp")
    shard_self = lax.axis_index("mp")
    rows_here = features.shape[0]
    side = tiles.shape[4]
    cb_dev = features.shape[1] // side
    fan = tiles.shape[2]
    per_peer = cb_dev * fan // shard_count
    layer_total = tiles.shape[0]
    current = features
    for layer_no in range(layer_total):
        table = in_block[layer_no].reshape(shard_count, shard_count, per_peer)
        blocks_here = current.reshape(rows_here, cb_dev, side)
        wanted = (
            lax.dynamic_index_in_dim(table, shard_self, 1, False).reshape(-1) - shard_self * cb_dev
        )
        outgoing = jnp.take(blocks_here, wanted, axis=1)
        incoming = lax.all_to_all(outgoing, "mp", split_axis=1, concat_axis=1, tiled=True)
        inputs = incoming.reshape(rows_here, cb_dev, fan, side)
        layer_tiles = lax.all_gather(tiles[layer_no], "batch", axis=2, tiled=True)
        total = jnp.einsum(
            "rjki,jkio->rjo", inputs, layer_tiles, preferred_element_type=jnp.float32
        )
        shifted = total + biases[layer_no].reshape(cb_dev, side)[None, :, :]
        current = (
            jnp.clip(shifted, 0.0, 32.0).astype(jnp.bfloat16).reshape(rows_here, cb_dev * side)
        )
    partial_sum = jnp.sum(current.astype(jnp.float32), axis=1)
    row_means = lax.psum(partial_sum, "mp") / NEUR
    grand = lax.psum(jnp.sum(row_means), "batch") / (rows_here * lax.axis_size("batch"))
    return (current, row_means, grand)


def solution(mesh):
    placed = (P("batch", "mp"), P(None, "mp", None, "batch", None), P(None, "mp"), P())
    return jax.shard_map(
        on_device,
        mesh=mesh,
        in_specs=placed,
        out_specs=(P("batch", "mp"), P("batch"), P()),
        check_vma=False,
    )
```

profile of v0, /device:TPU:0, one launch (start us, length us, event | category | flops | bytes accessed | tf_op | source)
XLA Modules:
  0.0 444.5 jit_solution(14762119534052150000)
XLA Ops:
  7.2 3.6 fusion.15
  10.8 6.4 %copy.25 = bf16[128,16384]{0,1:T(8,128)(2,1)} copy(bf16[128,16384]{1,0:T(8,128)(2,1)} %param.6) | data formatting | bytes 8388608 | tf_op args[0]
  17.2 6.5 %copy.26 = bf16[128,128,128]{2,0,1:T(8,128)(2,1)} copy(bf16[128,128,128]{0,2,1:T(8,128)(2,1)} %bitcast.46) | data formatting | bytes 8388608 | tf_op jit(solution)/shard_map/reshape | solution.py:21
  23.8 0.2 reshape_squeeze.7
  24.0 0.1 copy.24
  24.2 0.2 reshape_squeeze.6
  24.5 13.6 %gather_fusion = bf16[384,128,128]{2,1,0:T(8,128)(2,1)} fusion(bf16[128,128,128]{2,0,1:T(8,128)(2,1)} %copy.26, s32[1024]{0:T(1024)S(1)} %pad_clamp_fusion.1), kind=kCustom, calls=%fused_computation.clone | custom fusion | bytes 25167360 | tf_op jit(solution)/shard_map/jit(_take)/gather | solution.py:25
  38.1 11.0 %select_bitcast_fusion.1 = bf16[128,384,128]{2,0,1:T(8,128)(2,1)} fusion(bf16[384,128,128]{2,1,0:T(8,128)(2,1)} %gather_fusion, pred[384]{0:T(512)(128)(4,1)S(1)} %compare_and_fusion.1), kind=kLoop, calls=%fused_computation.7 | loop fusion | flops 6291456 | bytes 25166208 | tf_op jit(solution)/shard_map/jit(_take)/select_n | solution.py:25
  49.1 6.6 %all-to-all-start = ((bf16[128,384,128]{2,0,1:T(8,128)(2,1)}), bf16[128,384,128]{2,0,1:T(8,128)(2,1)}, u32[]{:S(2)}, u32[]{:S(2)}) async-start(bf16[128,384,128]{2,0,1:T(8,128)(2,1)} %select_bitcast_fusion.1), calls=%async_computation | async-start | bytes 25165824 | tf_op jit(solution)/shard_map/all_to_all | solution.py:26
  55.7 0.2 all-gather.7.cloned.1.call-start
  55.9 1.6 copy.35
  57.7 136.7 %all-to-all-done = bf16[128,384,128]{2,0,1:T(8,128)(2,1)} async-done(((bf16[128,384,128]{2,0,1:T(8,128)(2,1)}), bf16[128,384,128]{2,0,1:T(8,128)(2,1)}, u32[]{:S(2)}, u32[]{:S(2)}) %all-to-all-start) | async-done | bytes 12582944 | tf_op jit(solution)/shard_map/all_to_all | solution.py:26
  194.4 15.2 %fusion.8 = bf16[128,128,128]{2,0,1:T(8,128)(2,1)} fusion(f32[128,128]{1,0:T(8,128)S(1)} %bitcast.48, bf16[128,128,3,128]{3,0,2,1:T(8,128)(2,1)} %bitcast.2, bf16[1,128,3,128,128]{4,3,2,1,0:T(8,128)(2,1)} %all-gather.5.cloned.1.call-done), kind=kOutput, calls=%fused_computation.15 | convolution fusion | flops 1616904192 | bytes 29425664 | tf_op jit(solution)/shard_map/rjki,jkio->rjo/dot_general | solution.py:29
  209.6 13.5 %gather_fusion.1 = bf16[384,128,128]{2,1,0:T(8,128)(2,1)} fusion(bf16[128,128,128]{2,0,1:T(8,128)(2,1)} %fusion.8, s32[1024]{0:T(1024)S(1)} %pad_clamp_fusion), kind=kCustom, calls=%fused_computation.1.clone | custom fusion | bytes 25167360 | tf_op jit(solution)/shard_map/jit(_take)/gather | solution.py:25
  223.1 11.0 %select_bitcast_fusion = bf16[128,384,128]{2,0,1:T(8,128)(2,1)} fusion(bf16[384,128,128]{2,1,0:T(8,128)(2,1)} %gather_fusion.1, pred[384]{0:T(512)(128)(4,1)S(1)} %compare_and_fusion), kind=kLoop, calls=%fused_computation.6 | loop fusion | flops 6291456 | bytes 25166208 | tf_op jit(solution)/shard_map/jit(_take)/select_n | solution.py:25
  234.1 6.3 %all-to-all-start.1 = ((bf16[128,384,128]{2,0,1:T(8,128)(2,1)}), bf16[128,384,128]{2,0,1:T(8,128)(2,1)}, u32[]{:S(2)}, u32[]{:S(2)}) async-start(bf16[128,384,128]{2,0,1:T(8,128)(2,1)} %select_bitcast_fusion), calls=%async_computation.1 | async-start | bytes 25165824 | tf_op jit(solution)/shard_map/all_to_all | solution.py:26
  240.4 125.9 %all-gather.7.cloned.1.call-done = bf16[1,128,3,128,128]{4,1,2,0,3:T(8,128)(2,1)} async-done(((bf16[1,128,3,16,128]{4,1,2,0,3:T(8,128)(2,1)}), bf16[1,128,3,128,128]{4,1,2,0,3:T(8,128)(2,1)}) %all-gather.7.cloned.1.call-update) | async-done | bytes 12582928 | tf_op jit(solution)/shard_map/all_gather | solution.py:28
  366.3 17.6 %copy.28 = bf16[1,128,3,128,128]{3,4,2,1,0:T(8,128)(2,1)} copy(bf16[1,128,3,128,128]{4,1,2,0,3:T(8,128)(2,1)} %all-gather.7.cloned.1.call-done) | data formatting | bytes 25165824 | tf_op jit(solution)/shard_map/all_gather | solution.py:28
  383.9 12.4 %convert_reduce_fusion = (f32[128]{0:T(128)S(1)}, bf16[128,128,128]{2,0,1:T(8,128)(2,1)}) fusion(f32[128,128]{1,0:T(8,128)S(1)} %bitcast.47, bf16[128,128,3,128]{3,0,2,1:T(8,128)(2,1)} %bitcast.9, bf16[1,128,3,128,128]{3,4,2,1,0:T(8,128)(2,1)} %copy.28), kind=kOutput, calls=%fused_computation.14 | convolution fusion | flops 1621098368 | bytes 29426176 | tf_op jit(solution)/shard_map/rjki,jkio->rjo/dot_general | solution.py:29
  396.3 6.4 %copy.30 = bf16[128,128,128]{0,2,1:T(8,128)(2,1)} copy(bf16[128,128,128]{2,0,1:T(8,128)(2,1)} %get-tuple-element.22) | data formatting | bytes 8388608 | tf_op jit(solution)/shard_map/convert_element_type | solution.py:34
  402.6 6.4 %copy.31 = bf16[128,16384]{1,0:T(8,128)(2,1)} copy(bf16[128,16384]{0,1:T(8,128)(2,1)} %bitcast.45) | data formatting | bytes 8388608
  409.0 5.7 %psum.14 = f32[128]{0:T(128)S(1)} all-reduce(f32[128]{0:T(128)S(1)} %get-tuple-element.21), channel_id=1, replica_groups=mesh['batch'=8,'mp'=4] {'mp'}, use_global_device_ids=true, to_apply=%region_1.3 | all-reduce | flops 128 | bytes 1024 | tf_op jit(solution)/shard_map/psum | solution.py:37
  414.7 1.1 fusion.14
  415.8 20.1 %psum.15 = f32[]{:T(128)} all-reduce(f32[]{:T(128)} %get-tuple-element.13), channel_id=1, replica_groups=mesh['batch'=8,'mp'=4] {'batch'}, use_global_device_ids=true, to_apply=%region_3.5 | all-reduce | flops 1 | bytes 8 | tf_op jit(solution)/shard_map/psum | solution.py:38
  (21 shorter events, 0.6 us)
Async XLA Ops:
  7.2 16.5 %copy-start.1 = (s32[2,512,3]{1,0,2:T(2,128)S(1)}, s32[2,512,3]{1,0,2:T(2,128)}, u32[]{:S(2)}) copy-start(s32[2,512,3]{1,0,2:T(2,128)} %param.9) | copy-start | bytes 36868
  7.2 187.2 %all-gather.5.cloned.1.call-start = ((), (), s32[]{:S(2)}) async-start(), calls=%async_computation.2 | async-start | bytes 14155776 | tf_op jit(solution)/shard_map/all_gather | solution.py:28
  49.1 8.5 %copy-start = (f32[2,16384]{1,0:T(2,128)S(1)}, f32[2,16384]{1,0:T(2,128)}, u32[]{:S(2)}) copy-start(f32[2,16384]{1,0:T(2,128)} %param.8) | copy-start | bytes 393220
  49.1 145.3 %all-to-all-start = ((bf16[128,384,128]{2,0,1:T(8,128)(2,1)}), bf16[128,384,128]{2,0,1:T(8,128)(2,1)}, u32[]{:S(2)}, u32[]{:S(2)}) async-start(bf16[128,384,128]{2,0,1:T(8,128)(2,1)} %select_bitcast_fusion.1), calls=%async_computation | async-start | bytes 25165824 | tf_op jit(solution)/shard_map/all_to_all | solution.py:26
  55.7 310.6 %all-gather.7.cloned.1.call-start = ((), (), s32[]{:S(2)}) async-start(), calls=%async_computation.3 | async-start | bytes 14155776 | tf_op jit(solution)/shard_map/all_gather | solution.py:28
  234.1 149.8 %all-to-all-start.1 = ((bf16[128,384,128]{2,0,1:T(8,128)(2,1)}), bf16[128,384,128]{2,0,1:T(8,128)(2,1)}, u32[]{:S(2)}, u32[]{:S(2)}) async-start(bf16[128,384,128]{2,0,1:T(8,128)(2,1)} %select_bitcast_fusion), calls=%async_computation.1 | async-start | bytes 25165824 | tf_op jit(solution)/shard_map/all_to_all | solution.py:26
Sparse Core Ops, SparseCore 0:
  10.9 178.8 all-gather.4
  192.0 174.2 all-gather.6
where the time goes:
time: 446 us; the launch traced here: 445 us
  waiting for transfers between devices  263 us (59%)
  local copies, waits for them, and re-layouts  76.3 us (17%)
  matrix products  27.6 us (6%)
  blocking collectives  25.8 us (6%)
  other arithmetic  23.2 us (5%)
  between operations  15.9 us (4%)
  starting transfers between devices  13.2 us (3%)
    all_to_all x2, waiting for transfers between devices, on_device(): lax.all_to_all(outgoing, 'mp', split_axis=1, concat_axis=1, tiled=True)  137 us
    all_gather x2, waiting for transfers between devices, on_device(): layer_tiles = lax.all_gather(tiles[layer_no], 'batch', axis=2, tiled=True)  126 us
    dot_general x2, matrix products, on_device(): jnp.einsum('rjki,jkio->rjo', inputs, layer_tiles, preferred_element_type=...  27.6 us
    gather x2, local copies, waits for them, and re-layouts, on_device(): outgoing = jnp.take(blocks_here, wanted, axis=1)  27.1 us
    select_n x4, other arithmetic, on_device(): outgoing = jnp.take(blocks_here, wanted, axis=1)  22 us
    psum x1, blocking collectives, on_device(): lax.psum(jnp.sum(row_means), 'batch') / (rows_here * lax.axis_size('batch'))  20.1 us
    all_gather x1, local copies, waits for them, and re-layouts, on_device(): layer_tiles = lax.all_gather(tiles[layer_no], 'batch', axis=2, tiled=True)  17.6 us
    unnamed x7, local copies, waits for them, and re-layouts  14.3 us
  transfers between devices with their start and end apart: 4, of which 2 were waited for; matrix products, arithmetic and copies ran while one was open for 22% of the time, Pallas kernels for 0%

commit v1 on v0

v1 whole, which is shorter than its diff:
```python
import functools

import jax
import jax.numpy as jnp
from jax import lax
from jax.experimental import pallas as pl
from jax.experimental.pallas import tpu as pltpu
from jax.sharding import PartitionSpec as P

MESH = pl.DeviceIdType.MESH


def geometry(mesh):
    groups, shards = mesh.devices.shape
    where = [getattr(d, "coords", None) for d in mesh.devices[:, 0]]
    if groups == 1 or where[0] is None or where[0] == where[1]:
        return groups, 1, True, 1
    moved = [i for i in range(len(where[0])) if where[0][i] != where[1][i]][0]
    minor = 1
    while minor < groups and all(
        where[minor][i] == where[0][i] for i in range(len(where[0])) if i != moved
    ):
        minor += 1
    major = groups // minor
    row = [d.coords for d in mesh.devices[0, :]]
    cores = sum(1 for c in row if c == row[0])
    if major >= minor:
        return major, minor, True, cores
    return minor, major, False, cores


def gather_kernel(
    geo, shards, layer, pieces,
    tiles, cur, wout, xout,
    wv, xv, lsem, wrecv, wup, wdn, wcross, whalf, xrecv, xfar, xcore,
):
    nl, nq, line_major, nc = geo
    ny = shards // nc
    bi = lax.axis_index("batch")
    mi = lax.axis_index("mp")
    if line_major:
        l, q = bi // nq, bi % nq
    else:
        l, q = bi % nl, bi // nl
    y, core = mi // nc, mi % nc
    step_w = tiles.shape[1] // pieces
    step_x = cur.shape[0] // pieces
    halves = nq == 2 and nl % 2 == 0
    first = pieces // 2

    def group(level, side):
        return level * nq + side if line_major else side * nl + level

    sides = [(q + d) % nq for d in range(1, nq)]
    fars = [((y + d) % ny) * nc + core for d in range(1, ny)]
    partners = [y * nc + (core + d) % nc for d in range(1, nc)]

    barrier = pltpu.get_barrier_semaphore()

    def greet(b, m):
        pl.semaphore_signal(barrier, inc=1, device_id=(b, m), device_id_type=MESH)

    @pl.when(l > 0)
    def _():
        greet(group(l - 1, q), mi)

    @pl.when(l < nl - 1)
    def _():
        greet(group(l + 1, q), mi)

    for side in sides:
        greet(group(l, side), mi)
    for m in fars + partners:
        greet(bi, m)
    near = jnp.where(l > 0, 1, 0) + jnp.where(l < nl - 1, 1, 0)
    pl.semaphore_wait(barrier, len(sides) + len(fars) + len(partners) + near)

    in_w = pltpu.make_async_copy(tiles.at[layer], wv, lsem.at[0])
    in_x = pltpu.make_async_copy(cur, xv, lsem.at[1])
    in_w.start()
    in_x.start()

    def wcopy(own, b, c, to, ssem):
        part = pl.ds(c * step_w, step_w)
        return pltpu.make_async_remote_copy(
            src_ref=tiles.at[layer, part] if own else wout.at[b, part],
            dst_ref=wout.at[b, part],
            send_sem=ssem,
            recv_sem=wrecv.at[b, c],
            device_id=(to, mi),
            device_id_type=MESH,
        )

    def xcopy(own, m, c, to, ssem):
        part = pl.ds(c * step_x, step_x)
        return pltpu.make_async_remote_copy(
            src_ref=cur.at[part] if own else xout.at[m, part],
            dst_ref=xout.at[m, part],
            send_sem=ssem,
            recv_sem=xrecv.at[m, c],
            device_id=(bi, to),
            device_id_type=MESH,
        )

    def phase(p, c, drain):
        def go(copy):
            copy.wait_send() if drain else copy.start()

        def arrived_w(b):
            if not drain:
                wcopy(False, b, c, bi, wup.at[0, c]).wait_recv()

        if p == 0:
            @pl.when(l < nl - 1)
            def _():
                go(wcopy(True, bi, c, group(l + 1, q), wup.at[0, c]))

            @pl.when(l > 0)
            def _():
                go(wcopy(True, bi, c, group(l - 1, q), wdn.at[0, c]))

            for i, side in enumerate(sides):
                go(wcopy(True, bi, c, group(l, side), wcross.at[i, l, c]))
            for i, m in enumerate(fars):
                go(xcopy(True, mi, c, m, xfar.at[i, c]))
            for i, m in enumerate(partners):
                go(xcopy(True, mi, c, m, xcore.at[i, y, c]))
        else:
            @pl.when(l - p >= 0)
            def _():
                b = group(l - p, q)
                arrived_w(b)

                @pl.when(l < nl - 1)
                def _():
                    go(wcopy(False, b, c, group(l + 1, q), wup.at[p, c]))

                def across():
                    for i, side in enumerate(sides):
                        go(wcopy(False, b, c, group(l, side), wcross.at[i, l - p, c]))

                if halves and p == 1:
                    pl.when((l < nl // 2) | (c < first))(across)
                else:
                    across()

            @pl.when(l + p <= nl - 1)
            def _():
                b = group(l + p, q)
                arrived_w(b)

                @pl.when(l > 0)
                def _():
                    go(wcopy(False, b, c, group(l - 1, q), wdn.at[p, c]))

                def across():
                    for i, side in enumerate(sides):
                        go(wcopy(False, b, c, group(l, side), wcross.at[i, l + p, c]))

                if halves and p == 1:
                    pl.when((l >= nl // 2) | (c < first))(across)
                else:
                    across()

            if halves and p == 1:
                @pl.when(c >= first)
                def _():
                    b = group(l, sides[0])
                    arrived_w(b)

                    @pl.when((l + 1 >= nl // 2) & (l < nl - 1))
                    def _():
                        go(wcopy(False, b, c, group(l + 1, q), whalf.at[0, c]))

                    @pl.when((l - 1 < nl // 2) & (l > 0))
                    def _():
                        go(wcopy(False, b, c, group(l - 1, q), whalf.at[1, c]))

        if p == nl - 1:
            for d, far in enumerate(fars):
                if not drain:
                    xcopy(False, far, c, mi, xfar.at[0, c]).wait_recv()
                for i, m in enumerate(partners):
                    go(xcopy(False, far, c, m, xcore.at[i, far // nc, c]))

    for p in range(nl):
        @pl.loop(0, pieces)
        def _(c, p=p):
            phase(p, c, False)

        if p == 0:
            in_w.wait()
            in_x.wait()
            out_w = pltpu.make_async_copy(wv, wout.at[bi], lsem.at[2])
            out_x = pltpu.make_async_copy(xv, xout.at[mi], lsem.at[3])
            out_w.start()
            out_x.start()

    @pl.loop(0, pieces)
    def _(c):
        for side in sides:
            for level in range(nl):
                b = group(level, side)

                def arrive(b=b):
                    wcopy(False, b, c, bi, wup.at[0, c]).wait_recv()

                if halves:
                    pl.when((l != level) | (c < first))(arrive)
                else:
                    arrive()
        for m in partners:
            for yy in range(ny):
                xcopy(False, yy * nc + m % nc, c, mi, xfar.at[0, c]).wait_recv()

    out_w.wait()
    out_x.wait()
    for p in range(nl):
        @pl.loop(0, pieces)
        def _(c, p=p):
            phase(p, c, True)


def gather(geo, shards, groups, layer, tiles, cur):
    nl, nq, _, nc = geo
    pieces = 8 if groups <= 8 else 2
    ny = shards // nc
    dma = pltpu.SemaphoreType.DMA
    return pl.pallas_call(
        functools.partial(gather_kernel, geo, shards, layer, pieces),
        out_shape=(
            jax.ShapeDtypeStruct((groups,) + tiles.shape[1:], tiles.dtype),
            jax.ShapeDtypeStruct((shards,) + cur.shape, cur.dtype),
        ),
        in_specs=[pl.BlockSpec(memory_space=pl.ANY)] * 2,
        out_specs=(pl.BlockSpec(memory_space=pl.ANY),) * 2,
        scratch_shapes=[
            pltpu.VMEM(tiles.shape[1:], tiles.dtype),
            pltpu.VMEM(cur.shape, cur.dtype),
            dma((4,)),
            dma((groups, pieces)),
            dma((nl, pieces)),
            dma((nl, pieces)),
            dma((max(nq - 1, 1), nl, pieces)),
            dma((2, pieces)),
            dma((shards, pieces)),
            dma((max(ny - 1, 1), pieces)),
            dma((max(nc - 1, 1), ny, pieces)),
        ],
        compiler_params=pltpu.CompilerParams(collective_id=layer, has_side_effects=True),
        name=f"gather_{layer}",
    )(tiles, cur)


def layer_kernel(fan, batch_blocks, steps, ids, x_ref, w_ref, b_ref, o_ref, s_ref):
    step = pl.program_id(0) * steps + pl.program_id(1)
    side = w_ref.shape[4]

    @pl.when(step == 0)
    def _():
        s_ref[...] = jnp.zeros_like(s_ref)

    for j in range(batch_blocks):
        xs, ws = [], []
        for t in range(fan):
            at = ids[(step * batch_blocks + j) * fan + t]
            xs.append(x_ref[0, :, pl.ds(pl.multiple_of(at * side, side), side)])
            ws.append(w_ref[:, j, t].reshape(side, side))
        total = jnp.dot(
            jnp.concatenate(xs, axis=1),
            jnp.concatenate(ws, axis=0),
            preferred_element_type=jnp.float32,
        )
        cols = slice(j * side, (j + 1) * side)
        out = jnp.clip(total + b_ref[:, cols], 0.0, 32.0).astype(o_ref.dtype)
        o_ref[:, cols] = out
        s_ref[...] += out.astype(jnp.float32)


def apply_layer(ids, xall, wall, bias, blocks):
    shards, rows, width = xall.shape
    groups, cb, fan, share, side = wall.shape
    per_shard = cb // shards
    batch_blocks = min(blocks, per_shard)
    steps = per_shard // batch_blocks
    return pl.pallas_call(
        functools.partial(layer_kernel, fan, batch_blocks, steps),
        out_shape=(
            jax.ShapeDtypeStruct((rows, width), xall.dtype),
            jax.ShapeDtypeStruct((rows, side), jnp.float32),
        ),
        grid_spec=pltpu.PrefetchScalarGridSpec(
            num_scalar_prefetch=1,
            grid=(shards, steps),
            in_specs=[
                pl.BlockSpec((1, rows, width), lambda s, k, ids: (s, 0, 0)),
                pl.BlockSpec(
                    (groups, batch_blocks, fan, share, side),
                    lambda s, k, ids: (0, s * steps + k, 0, 0, 0),
                ),
                pl.BlockSpec((1, batch_blocks * side), lambda s, k, ids: (0, s * steps + k)),
            ],
            out_specs=(
                pl.BlockSpec((rows, batch_blocks * side), lambda s, k, ids: (0, s * steps + k)),
                pl.BlockSpec((rows, side), lambda s, k, ids: (0, 0)),
            ),
        ),
        compiler_params=pltpu.CompilerParams(
            dimension_semantics=("arbitrary", "arbitrary"), vmem_limit_bytes=48 * 1024 * 1024
        ),
    )(ids, xall, wall, bias)


def on_device(geo, features, tiles, biases, in_block):
    shards = lax.axis_size("mp")
    groups = lax.axis_size("batch")
    me = lax.axis_index("mp")
    rows = features.shape[0]
    side = tiles.shape[4]
    cb = tiles.shape[1]
    fan = tiles.shape[2]
    current = features
    mine = lax.dynamic_slice_in_dim(in_block, me * cb, cb, axis=1) % cb
    for layer in range(tiles.shape[0]):
        wall, xall = gather(geo, shards, groups, layer, tiles, current)
        current, sums = apply_layer(
            mine[layer].reshape(-1), xall, wall, biases[layer].reshape(1, -1), 8
        )
    spot = (jnp.arange(groups) == lax.axis_index("batch")).astype(jnp.float32)
    everyone = lax.psum(spot[:, None] * jnp.sum(sums, axis=1)[None, :], ("batch", "mp"))
    neurons = cb * side * shards
    row_means = (
        lax.dynamic_index_in_dim(everyone, lax.axis_index("batch"), 0, False) / neurons
    )
    grand = jnp.sum(everyone / neurons) / (rows * groups)
    return (current, row_means, grand)


def solution(mesh):
    placed = (P("batch", "mp"), P(None, "mp", None, "batch", None), P(None, "mp"), P())
    return jax.shard_map(
        functools.partial(on_device, geometry(mesh)),
        mesh=mesh,
        in_specs=placed,
        out_specs=(P("batch", "mp"), P("batch"), P()),
        check_vma=False,
    )
```

time: 446 us -> 349 us (0.78)
  Pallas kernels: 0 us -> 302 us
  waiting for transfers between devices: 263 us -> 0 us
  local copies, waits for them, and re-layouts: 76.3 us -> 3.75 us
  matrix products: 27.6 us -> 0 us
  other arithmetic: 23.2 us -> 1.99 us
  between operations: 15.9 us -> 2.47 us
  starting transfers between devices: 13.2 us -> 0 us
  blocking collectives: 25.8 us -> 38.7 us
    pallas_call x0 -> x4, Pallas kernels: none -> 302 us  [the longest x2 262 us: gather(): pl.pallas_call(functools.partial(gather_kernel, geo, shards, layer, piece...]
    all_to_all x2 -> x0, waiting for transfers between devices: 137 us -> none  [on_device(): lax.all_to_all(outgoing, 'mp', split_axis=1, concat_axis=1, tiled=True)]
    all_gather x2 -> x0, waiting for transfers between devices: 126 us -> none  [on_device(): layer_tiles = lax.all_gather(tiles[layer_no], 'batch', axis=2, tiled=True)]
    dot_general x2 -> x0, matrix products: 27.6 us -> none  [on_device(): jnp.einsum('rjki,jkio->rjo', inputs, layer_tiles, preferred_element_type=...]
    gather x2 -> x0, local copies, waits for them, and re-layouts: 27.1 us -> none  [on_device(): outgoing = jnp.take(blocks_here, wanted, axis=1)]
    select_n x4 -> x1, other arithmetic: 22 us -> 0.7 us  [on_device(): mine = lax.dynamic_slice_in_dim(in_block, me * cb, cb, axis=1) % cb]
    all_gather x1 -> x0, local copies, waits for them, and re-layouts: 17.6 us -> none  [on_device(): layer_tiles = lax.all_gather(tiles[layer_no], 'batch', axis=2, tiled=True)]
    all_to_all x2 -> x0, starting transfers between devices: 12.9 us -> none  [on_device(): lax.all_to_all(outgoing, 'mp', split_axis=1, concat_axis=1, tiled=True)]
  transfers between devices with their start and end apart: 4 -> 0, of which waited for: 2 -> 0; matrix products, arithmetic and copies ran while one was open for 22% -> 0% of each run, Pallas kernels for 0% -> 0%
where the time goes in v1:
time: 349 us; the launch traced here: 348 us
  Pallas kernels  302 us (87%)
  blocking collectives  38.7 us (11%)
  local copies, waits for them, and re-layouts  3.75 us (1%)
    pallas_call x2, Pallas kernels, gather(): pl.pallas_call(functools.partial(gather_kernel, geo, shards, layer, piece...  262 us
    pallas_call x2, Pallas kernels, apply_layer(): pl.pallas_call(functools.partial(layer_kernel, fan, batch_blocks, steps),...  39.7 us
    psum x1, blocking collectives, on_device(): lax.psum(spot[:, None] * jnp.sum(sums, axis=1)[None, :], ('batch', 'mp'))  38.7 us

profile of v1, /device:TPU:0, one launch (start us, length us, event | category | flops | bytes accessed | tf_op | source)
XLA Modules:
  0.0 348.5 jit_solution(8027697478736580611)
XLA Ops:
  0.6 0.7 and_select_fusion
  1.3 0.1 copy.8
  1.5 0.2 reshape_squeeze.7.ids
  1.7 132.8 %gather_0.1 = (bf16[8,128,3,16,128]{4,3,2,1,0:T(8,128)(2,1)}, bf16[4,128,16384]{2,1,0:T(8,128)(2,1)}) custom-call(bf16[2,128,3,16,128]{4,3,2,1,0:T(8,128)(2,1)} %tiles.3, bf16[128,16384]{1,0:T(8,128)(2,1)} %cur.1), custom_call_target="tpu_custom_call" | custom-call | tf_op jit(solution)/shard_map/gather_0/pallas_call | solution.py:229
  134.4 1.1 fusion.1
  135.5 19.3 %shard_map.67 = (bf16[128,16384]{1,0:T(8,128)(2,1)S(1)}, f32[128,128]{1,0:T(8,128)}) custom-call(s32[384]{0:T(512)S(1)} %reshape_squeeze.7.ids, bf16[4,128,16384]{2,1,0:T(8,128)(2,1)} %get-tuple-element.10.x_ref, bf16[8,128,3,16,128]{4,3,2,1,0:T(8,128)(2,1)} %get-tuple-element.11.w_ref, f32[1,16384]{1,0:T(1,128)S(1)} %get-tuple-element.18.b_ref), custom_call_target="tpu_custom_call" | custom-call | tf_op jit(solution)/shard_map/pallas_call | solution.py:286
  154.8 0.0 copy-start
  154.8 2.0 copy-done
  156.8 129.2 %gather_1.1 = (bf16[8,128,3,16,128]{4,3,2,1,0:T(8,128)(2,1)}, bf16[4,128,16384]{2,1,0:T(8,128)(2,1)}) custom-call(bf16[2,128,3,16,128]{4,3,2,1,0:T(8,128)(2,1)} %tiles.3, bf16[128,16384]{1,0:T(8,128)(2,1)} %copy-done), custom_call_target="tpu_custom_call" | custom-call | tf_op jit(solution)/shard_map/gather_1/pallas_call | solution.py:229
  286.0 0.1 copy.7
  286.1 0.2 reshape_squeeze.6.ids
  286.3 20.4 %shard_map.68 = (bf16[128,16384]{1,0:T(8,128)(2,1)}, f32[128,128]{1,0:T(8,128)S(1)}) custom-call(s32[384]{0:T(512)S(1)} %reshape_squeeze.6.ids, bf16[4,128,16384]{2,1,0:T(8,128)(2,1)} %get-tuple-element.13.x_ref, bf16[8,128,3,16,128]{4,3,2,1,0:T(8,128)(2,1)} %get-tuple-element.14.w_ref, f32[1,16384]{1,0:T(1,128)S(1)} %get-tuple-element.17.b_ref), custom_call_target="tpu_custom_call" | custom-call | tf_op jit(solution)/shard_map/pallas_call | solution.py:286
  306.7 0.1 reduce_sum.18
  306.8 0.1 broadcast_multiply_fusion
  306.9 38.7 %psum.7 = f32[8,128]{1,0:T(8,128)S(1)} all-reduce(f32[8,128]{1,0:T(8,128)S(1)} %broadcast_multiply_fusion), channel_id=1, replica_groups=mesh['batch'=8,'mp'=4] {'batch','mp'}, use_global_device_ids=true, to_apply=%region_1.2 | all-reduce | flops 1024 | bytes 8192 | tf_op jit(solution)/shard_map/psum | solution.py:330
  345.6 0.5 multiply_bitcast_fusion
  346.1 0.6 multiply_reduce_fusion
  (2 shorter events, 0.0 us)
Async XLA Ops:
  154.8 2.0 copy-start

commit v2 on v1

--- a/solution.py
+++ b/solution.py
@@ -252,7 +252,7 @@
     )(tiles, cur)
 
 
-def layer_kernel(fan, batch_blocks, steps, ids, x_ref, w_ref, b_ref, o_ref, s_ref):
+def layer_kernel(fan, batch_blocks, steps, ids, x_ref, w_ref, b_ref, o_ref, r_ref, s_ref):
     step = pl.program_id(0) * steps + pl.program_id(1)
     side = w_ref.shape[4]
 
@@ -276,6 +276,11 @@
         o_ref[:, cols] = out
         s_ref[...] += out.astype(jnp.float32)
 
+    @pl.when(step == pl.num_programs(0) * steps - 1)
+    def _():
+        line = jnp.sum(s_ref[...].T, axis=0, keepdims=True)
+        r_ref[...] = jnp.broadcast_to(line, r_ref.shape)
+
 
 def apply_layer(ids, xall, wall, bias, blocks):
     shards, rows, width = xall.shape
@@ -287,7 +292,7 @@
         functools.partial(layer_kernel, fan, batch_blocks, steps),
         out_shape=(
             jax.ShapeDtypeStruct((rows, width), xall.dtype),
-            jax.ShapeDtypeStruct((rows, side), jnp.float32),
+            jax.ShapeDtypeStruct((8, rows), jnp.float32),
         ),
         grid_spec=pltpu.PrefetchScalarGridSpec(
             num_scalar_prefetch=1,
@@ -302,13 +307,91 @@
             ],
             out_specs=(
                 pl.BlockSpec((rows, batch_blocks * side), lambda s, k, ids: (0, s * steps + k)),
-                pl.BlockSpec((rows, side), lambda s, k, ids: (0, 0)),
+                pl.BlockSpec((8, rows), lambda s, k, ids: (0, 0)),
             ),
+            scratch_shapes=[pltpu.VMEM((rows, side), jnp.float32)],
         ),
         compiler_params=pltpu.CompilerParams(
             dimension_semantics=("arbitrary", "arbitrary"), vmem_limit_bytes=48 * 1024 * 1024
         ),
     )(ids, xall, wall, bias)
+
+
+def means_kernel(groups, shards, neurons, x_ref, rows_ref, all_ref, slots, ssem, rsem):
+    bi = lax.axis_index("batch")
+    mi = lax.axis_index("mp")
+    me = bi * shards + mi
+    total = groups * shards
+    barrier = pltpu.get_barrier_semaphore()
+
+    def peer(d):
+        to = (me + d) % total
+        return to // shards, to % shards
+
+    @pl.loop(1, total)
+    def _(d):
+        pl.semaphore_signal(barrier, inc=1, device_id=peer(d), device_id_type=MESH)
+
+    pl.semaphore_wait(barrier, total - 1)
+
+    def copy(d, slot):
+        return pltpu.make_async_remote_copy(
+            src_ref=x_ref,
+            dst_ref=slots.at[slot],
+            send_sem=ssem.at[d],
+            recv_sem=rsem.at[slot],
+            device_id=peer(d),
+            device_id_type=MESH,
+        )
+
+    @pl.loop(1, total)
+    def _(d):
+        copy(d, me).start()
+
+    slots[me] = x_ref[...]
+
+    @pl.loop(1, total)
+    def _(d):
+        copy(d, (me + d) % total).wait_recv()
+
+    whole = jnp.zeros(all_ref.shape, jnp.float32)
+    for b in range(groups):
+        one = slots[b * shards]
+        for m in range(1, shards):
+            one = one + slots[b * shards + m]
+        whole = whole + one / neurons
+    all_ref[...] = whole
+    mine = slots[bi * shards]
+    for m in range(1, shards):
+        mine = mine + slots[bi * shards + m]
+    rows_ref[...] = mine / neurons
+
+    @pl.loop(1, total)
+    def _(d):
+        copy(d, me).wait_send()
+
+
+def means(groups, shards, neurons, sums):
+    total = groups * shards
+    if total > 64:
+        shard_sum = lax.psum(sums[0], "mp") / neurons
+        return shard_sum, lax.psum(shard_sum, "batch")
+    vmem = pl.BlockSpec(memory_space=pltpu.VMEM)
+    like = jax.ShapeDtypeStruct(sums.shape, jnp.float32)
+    mine, whole = pl.pallas_call(
+        functools.partial(means_kernel, groups, shards, neurons),
+        out_shape=(like, like),
+        in_specs=[vmem],
+        out_specs=(vmem, vmem),
+        scratch_shapes=[
+            pltpu.VMEM((total,) + sums.shape, jnp.float32),
+            pltpu.SemaphoreType.DMA((total,)),
+            pltpu.SemaphoreType.DMA((total,)),
+        ],
+        compiler_params=pltpu.CompilerParams(collective_id=20, has_side_effects=True),
+        name="means",
+    )(sums)
+    return mine[0], whole[0]
 
 
 def on_device(geo, features, tiles, biases, in_block):
@@ -326,13 +409,8 @@
         current, sums = apply_layer(
             mine[layer].reshape(-1), xall, wall, biases[layer].reshape(1, -1), 8
         )
-    spot = (jnp.arange(groups) == lax.axis_index("batch")).astype(jnp.float32)
-    everyone = lax.psum(spot[:, None] * jnp.sum(sums, axis=1)[None, :], ("batch", "mp"))
-    neurons = cb * side * shards
-    row_means = (
-        lax.dynamic_index_in_dim(everyone, lax.axis_index("batch"), 0, False) / neurons
-    )
-    grand = jnp.sum(everyone / neurons) / (rows * groups)
+    row_means, whole = means(groups, shards, cb * side * shards, sums)
+    grand = jnp.sum(whole) / (rows * groups)
     return (current, row_means, grand)
 
 

time: 349 us -> 322 us (0.923)
  blocking collectives: 38.7 us -> 0 us
  Pallas kernels: 302 us -> 312 us
    psum x1 -> x0, blocking collectives: 38.7 us -> none  [on_device(): lax.psum(spot[:, None] * jnp.sum(sums, axis=1)[None, :], ('batch', 'mp'))]
    pallas_call x0 -> x1, Pallas kernels: none -> 9.73 us  [means(): pl.pallas_call(functools.partial(means_kernel, groups, shards, neurons),...]
where the time goes in v2:
time: 322 us; the launch traced here: 321 us
  Pallas kernels  312 us (97%)
  local copies, waits for them, and re-layouts  5.52 us (2%)
    pallas_call x2, Pallas kernels, gather(): pl.pallas_call(functools.partial(gather_kernel, geo, shards, layer, piece...  262 us
    pallas_call x2, Pallas kernels, apply_layer(): pl.pallas_call(functools.partial(layer_kernel, fan, batch_blocks, steps),...  39.9 us
    pallas_call x1, Pallas kernels, means(): pl.pallas_call(functools.partial(means_kernel, groups, shards, neurons),...  9.73 us

profile of v2, /device:TPU:0, one launch (start us, length us, event | category | flops | bytes accessed | tf_op | source)
XLA Modules:
  0.0 321.5 jit_solution(12003945962301573122)
XLA Ops:
  0.6 0.7 and_select_fusion
  1.3 0.1 copy.8
  1.5 0.2 reshape_squeeze.7.ids
  1.7 132.8 %gather_0.1 = (bf16[8,128,3,16,128]{4,3,2,1,0:T(8,128)(2,1)}, bf16[4,128,16384]{2,1,0:T(8,128)(2,1)}) custom-call(bf16[2,128,3,16,128]{4,3,2,1,0:T(8,128)(2,1)} %tiles.3, bf16[128,16384]{1,0:T(8,128)(2,1)} %cur.1), custom_call_target="tpu_custom_call" | custom-call | tf_op jit(solution)/shard_map/gather_0/pallas_call | solution.py:229
  134.4 1.1 fusion.1
  135.5 19.4 %shard_map.67 = (bf16[128,16384]{1,0:T(8,128)(2,1)S(1)}, f32[8,128]{1,0:T(8,128)}) custom-call(s32[384]{0:T(512)S(1)} %reshape_squeeze.7.ids, bf16[4,128,16384]{2,1,0:T(8,128)(2,1)} %get-tuple-element.12.x_ref, bf16[8,128,3,16,128]{4,3,2,1,0:T(8,128)(2,1)} %get-tuple-element.13.w_ref, f32[1,16384]{1,0:T(1,128)S(1)} %get-tuple-element.22.b_ref), custom_call_target="tpu_custom_call" | custom-call | tf_op jit(solution)/shard_map/pallas_call | solution.py:291
  155.0 0.0 copy-start
  155.0 2.0 copy-done
  157.0 129.1 %gather_1.1 = (bf16[8,128,3,16,128]{4,3,2,1,0:T(8,128)(2,1)}, bf16[4,128,16384]{2,1,0:T(8,128)(2,1)}) custom-call(bf16[2,128,3,16,128]{4,3,2,1,0:T(8,128)(2,1)} %tiles.3, bf16[128,16384]{1,0:T(8,128)(2,1)} %copy-done), custom_call_target="tpu_custom_call" | custom-call | tf_op jit(solution)/shard_map/gather_1/pallas_call | solution.py:229
  286.1 0.1 copy.7
  286.2 0.2 reshape_squeeze.6.ids
  286.4 20.5 %shard_map.68 = (bf16[128,16384]{1,0:T(8,128)(2,1)}, f32[8,128]{1,0:T(8,128)S(1)}) custom-call(s32[384]{0:T(512)S(1)} %reshape_squeeze.6.ids, bf16[4,128,16384]{2,1,0:T(8,128)(2,1)} %get-tuple-element.15.x_ref, bf16[8,128,3,16,128]{4,3,2,1,0:T(8,128)(2,1)} %get-tuple-element.16.w_ref, f32[1,16384]{1,0:T(1,128)S(1)} %get-tuple-element.21.b_ref), custom_call_target="tpu_custom_call" | custom-call | tf_op jit(solution)/shard_map/pallas_call | solution.py:291
  306.9 0.0 copy-start.1
  306.9 0.6 copy-done.1
  307.5 9.7 %means.1 = (f32[8,128]{1,0:T(8,128)}, f32[8,128]{1,0:T(8,128)}) custom-call(f32[8,128]{1,0:T(8,128)} %copy-done.1), custom_call_target="tpu_custom_call" | custom-call | tf_op jit(solution)/shard_map/means/pallas_call | solution.py:381
  317.2 1.3 slice_reduce_fusion
  319.2 1.2 slice_bitcast_fusion
  (1 shorter events, 0.0 us)
Async XLA Ops:
  155.0 2.0 copy-start
  306.9 0.6 copy-start.1

commit v3 on v2

--- a/solution.py
+++ b/solution.py
@@ -1,4 +1,5 @@
 import functools
+import math
 
 import jax
 import jax.numpy as jnp
@@ -252,68 +253,74 @@
     )(tiles, cur)
 
 
-def layer_kernel(fan, batch_blocks, steps, ids, x_ref, w_ref, b_ref, o_ref, r_ref, s_ref):
-    step = pl.program_id(0) * steps + pl.program_id(1)
-    side = w_ref.shape[4]
-
-    @pl.when(step == 0)
-    def _():
-        s_ref[...] = jnp.zeros_like(s_ref)
-
-    for j in range(batch_blocks):
-        xs, ws = [], []
-        for t in range(fan):
-            at = ids[(step * batch_blocks + j) * fan + t]
-            xs.append(x_ref[0, :, pl.ds(pl.multiple_of(at * side, side), side)])
-            ws.append(w_ref[:, j, t].reshape(side, side))
-        total = jnp.dot(
-            jnp.concatenate(xs, axis=1),
-            jnp.concatenate(ws, axis=0),
-            preferred_element_type=jnp.float32,
+def layer_kernel(ids, x_ref, w_ref, b_ref, o_ref, r_ref, xl, wl, s_ref, loads):
+    shards, rows, _ = x_ref.shape
+    _, cb, fan, _, side = w_ref.shape
+    per_shard = cb // shards
+    width = math.gcd(per_shard, 8)
+
+    def pulls(s):
+        part = pl.ds(s * per_shard, per_shard)
+        return (
+            pltpu.make_async_copy(x_ref.at[s], xl.at[s], loads.at[0, s]),
+            pltpu.make_async_copy(w_ref.at[:, part], wl.at[:, part], loads.at[1, s]),
         )
-        cols = slice(j * side, (j + 1) * side)
-        out = jnp.clip(total + b_ref[:, cols], 0.0, 32.0).astype(o_ref.dtype)
-        o_ref[:, cols] = out
-        s_ref[...] += out.astype(jnp.float32)
-
-    @pl.when(step == pl.num_programs(0) * steps - 1)
-    def _():
-        line = jnp.sum(s_ref[...].T, axis=0, keepdims=True)
-        r_ref[...] = jnp.broadcast_to(line, r_ref.shape)
-
-
-def apply_layer(ids, xall, wall, bias, blocks):
+
+    for s in range(min(2, shards)):
+        for pull in pulls(s):
+            pull.start()
+    s_ref[...] = jnp.zeros_like(s_ref)
+    for s in range(shards):
+        for pull in pulls(s):
+            pull.wait()
+        if s + 2 < shards:
+            for pull in pulls(s + 2):
+                pull.start()
+
+        @pl.loop(0, per_shard // width)
+        def _(k, s=s):
+            for jj in range(width):
+                j = s * per_shard + k * width + jj
+                xs, ws = [], []
+                for t in range(fan):
+                    at = ids[j * fan + t]
+                    xs.append(xl[s, :, pl.ds(pl.multiple_of(at * side, side), side)])
+                    ws.append(wl[:, j, t].reshape(side, side))
+                total = jnp.dot(
+                    jnp.concatenate(xs, axis=1),
+                    jnp.concatenate(ws, axis=0),
+                    preferred_element_type=jnp.float32,
+                )
+                cols = pl.ds(pl.multiple_of(j * side, side), side)
+                out = jnp.clip(total + b_ref[:, cols], 0.0, 32.0).astype(o_ref.dtype)
+                o_ref[:, cols] = out
+                s_ref[...] += out.astype(jnp.float32)
+
+    line = jnp.sum(s_ref[...].T, axis=0, keepdims=True)
+    r_ref[...] = jnp.broadcast_to(line, r_ref.shape)
+
+
+def apply_layer(ids, xall, wall, bias):
     shards, rows, width = xall.shape
-    groups, cb, fan, share, side = wall.shape
-    per_shard = cb // shards
-    batch_blocks = min(blocks, per_shard)
-    steps = per_shard // batch_blocks
+    side = wall.shape[4]
+    hbm = pl.BlockSpec(memory_space=pl.ANY)
+    vmem = pl.BlockSpec(memory_space=pltpu.VMEM)
     return pl.pallas_call(
-        functools.partial(layer_kernel, fan, batch_blocks, steps),
+        layer_kernel,
         out_shape=(
             jax.ShapeDtypeStruct((rows, width), xall.dtype),
             jax.ShapeDtypeStruct((8, rows), jnp.float32),
         ),
-        grid_spec=pltpu.PrefetchScalarGridSpec(
-            num_scalar_prefetch=1,
-            grid=(shards, steps),
-            in_specs=[
-                pl.BlockSpec((1, rows, width), lambda s, k, ids: (s, 0, 0)),
-                pl.BlockSpec(
-                    (groups, batch_blocks, fan, share, side),
-                    lambda s, k, ids: (0, s * steps + k, 0, 0, 0),
-                ),
-                pl.BlockSpec((1, batch_blocks * side), lambda s, k, ids: (0, s * steps + k)),
-            ],
-            out_specs=(
-                pl.BlockSpec((rows, batch_blocks * side), lambda s, k, ids: (0, s * steps + k)),
-                pl.BlockSpec((8, rows), lambda s, k, ids: (0, 0)),
-            ),
-            scratch_shapes=[pltpu.VMEM((rows, side), jnp.float32)],
-        ),
-        compiler_params=pltpu.CompilerParams(
-            dimension_semantics=("arbitrary", "arbitrary"), vmem_limit_bytes=48 * 1024 * 1024
-        ),
+        in_specs=[pl.BlockSpec(memory_space=pltpu.SMEM), hbm, hbm, vmem],
+        out_specs=(vmem, vmem),
+        scratch_shapes=[
+            pltpu.VMEM(xall.shape, xall.dtype),
+            pltpu.VMEM(wall.shape, wall.dtype),
+            pltpu.VMEM((rows, side), jnp.float32),
+            pltpu.SemaphoreType.DMA((2, shards)),
+        ],
+        compiler_params=pltpu.CompilerParams(vmem_limit_bytes=52 * 1024 * 1024),
+        name="layer",
     )(ids, xall, wall, bias)
 
 
@@ -407,7 +414,7 @@
     for layer in range(tiles.shape[0]):
         wall, xall = gather(geo, shards, groups, layer, tiles, current)
         current, sums = apply_layer(
-            mine[layer].reshape(-1), xall, wall, biases[layer].reshape(1, -1), 8
+            mine[layer].reshape(-1), xall, wall, biases[layer].reshape(1, -1)
         )
     row_means, whole = means(groups, shards, cb * side * shards, sums)
     grand = jnp.sum(whole) / (rows * groups)

time: 322 us -> 308 us (0.957)
  Pallas kernels: 312 us -> 299 us
    pallas_call x2, Pallas kernels: 39.9 us -> 27.7 us  [apply_layer(): pl.pallas_call(layer_kernel, out_shape=(jax.ShapeDtypeStruct((rows, width...]
where the time goes in v3:
time: 308 us; the launch traced here: 307 us
  Pallas kernels  299 us (97%)
  local copies, waits for them, and re-layouts  3.52 us (1%)
    pallas_call x2, Pallas kernels, gather(): pl.pallas_call(functools.partial(gather_kernel, geo, shards, layer, piece...  262 us
    pallas_call x2, Pallas kernels, apply_layer(): pl.pallas_call(layer_kernel, out_shape=(jax.ShapeDtypeStruct((rows, width...  27.7 us
    pallas_call x1, Pallas kernels, means(): pl.pallas_call(functools.partial(means_kernel, groups, shards, neurons),...  9.72 us

profile of v3, /device:TPU:0, one launch (start us, length us, event | category | flops | bytes accessed | tf_op | source)
XLA Modules:
  0.0 307.3 jit_solution(18066144932089241264)
XLA Ops:
  0.6 0.7 and_select_fusion
  1.3 0.1 copy.8
  1.5 0.2 reshape_squeeze.7.ids
  1.7 132.8 %gather_0.1 = (bf16[8,128,3,16,128]{4,3,2,1,0:T(8,128)(2,1)}, bf16[4,128,16384]{2,1,0:T(8,128)(2,1)}) custom-call(bf16[2,128,3,16,128]{4,3,2,1,0:T(8,128)(2,1)} %tiles.3, bf16[128,16384]{1,0:T(8,128)(2,1)} %cur.1), custom_call_target="tpu_custom_call" | custom-call | tf_op jit(solution)/shard_map/gather_0/pallas_call | solution.py:230
  134.4 1.1 fusion.1
  135.5 13.8 %layer.2 = (bf16[128,16384]{1,0:T(8,128)(2,1)}, f32[8,128]{1,0:T(8,128)}) custom-call(s32[384]{0:T(512)S(1)} %reshape_squeeze.7.ids, bf16[4,128,16384]{2,1,0:T(8,128)(2,1)} %get-tuple-element.12.x_ref, bf16[8,128,3,16,128]{4,3,2,1,0:T(8,128)(2,1)} %get-tuple-element.13.w_ref, f32[1,16384]{1,0:T(1,128)S(1)} %get-tuple-element.22.b_ref), custom_call_target="tpu_custom_call" | custom-call | tf_op jit(solution)/shard_map/layer/pallas_call | solution.py:308
  149.4 129.2 %gather_1.1 = (bf16[8,128,3,16,128]{4,3,2,1,0:T(8,128)(2,1)}, bf16[4,128,16384]{2,1,0:T(8,128)(2,1)}) custom-call(bf16[2,128,3,16,128]{4,3,2,1,0:T(8,128)(2,1)} %tiles.3, bf16[128,16384]{1,0:T(8,128)(2,1)} %get-tuple-element.14.cur), custom_call_target="tpu_custom_call" | custom-call | tf_op jit(solution)/shard_map/gather_1/pallas_call | solution.py:230
  278.6 0.1 copy.7
  278.7 0.2 reshape_squeeze.6.ids
  278.9 13.8 %layer.3 = (bf16[128,16384]{1,0:T(8,128)(2,1)}, f32[8,128]{1,0:T(8,128)S(1)}) custom-call(s32[384]{0:T(512)S(1)} %reshape_squeeze.6.ids, bf16[4,128,16384]{2,1,0:T(8,128)(2,1)} %get-tuple-element.15.x_ref, bf16[8,128,3,16,128]{4,3,2,1,0:T(8,128)(2,1)} %get-tuple-element.16.w_ref, f32[1,16384]{1,0:T(1,128)S(1)} %get-tuple-element.21.b_ref), custom_call_target="tpu_custom_call" | custom-call | tf_op jit(solution)/shard_map/layer/pallas_call | solution.py:308
  292.8 0.0 copy-start
  292.8 0.6 copy-done
  293.3 9.7 %means.1 = (f32[8,128]{1,0:T(8,128)}, f32[8,128]{1,0:T(8,128)}) custom-call(f32[8,128]{1,0:T(8,128)} %copy-done), custom_call_target="tpu_custom_call" | custom-call | tf_op jit(solution)/shard_map/means/pallas_call | solution.py:388
  303.1 1.3 slice_reduce_fusion
  305.0 1.2 slice_bitcast_fusion
  (1 shorter events, 0.0 us)
Async XLA Ops:
  292.8 0.6 copy-start
